TPU v7x, 32 devices: a whole 2x2x4 slice. The times are simulated.
32 devices in a mesh: x: 4 (over z), yz: 8 (over y, x, core).
Axes of the slice: x: 2, y: 2, z: 4, core: 2. Of those that a mesh axis runs over, the one named last changes fastest.
Arguments:
- x_in: bfloat16 [512, 2048], P(None, ('x', 'yz'))
- ln_scale: float32 [2048], P(('x', 'yz'))
- w_gate_up: bfloat16 [2048, 2, 8192], P('x', None, 'yz')
- w_attn: bfloat16 [2048, 2304], P('x', 'yz')
- w_down: bfloat16 [8192, 2048], P('yz', 'x')
- w_out: bfloat16 [2048, 2048], P('yz', 'x')
- k_cache: bfloat16 [512, 2048, 128], P(('x', 'yz'))
- v_cache: bfloat16 [512, 2048, 128], P(('x', 'yz'))
- lengths: int32 [512], P(('x', 'yz'))
- positions: int32 [512], P(('x', 'yz'))
Outputs:
- output 1: bfloat16 [512, 2048], P(None, ('x', 'yz'))
- output 2: bfloat16 [512, 2048, 128], P(('x', 'yz'))
- output 3: bfloat16 [512, 2048, 128], P(('x', 'yz'))
All inputs are finite; a program needn't handle non-finite values.
Results may differ from a plain program's by a relative error of at most 0.00344997.
Values are sent between devices in bfloat16 or wider.
A program may use at most 1 GiB of HBM per device.

v0:
```python
import functools

import jax
import jax.numpy as jnp
from jax import lax
from jax.experimental import pallas as pl
from jax.experimental.pallas import tpu as pltpu
from jax.sharding import PartitionSpec as P

LN_EPS = 1e-6
ROPE_BASE = 10000.0
MESH = pl.DeviceIdType.MESH
F32 = jnp.float32
BF16 = jnp.bfloat16

NZ = 4
NP = 8
C1A = 16
C1 = 48
C2 = 128
C3 = 80
CA = C1 + C2
CHUNKS = 4
LANES = 512 // CHUNKS


def rotary(values, positions):
    half_dim = values.shape[-1] // 2
    inv_freq = ROPE_BASE ** (-jnp.arange(half_dim, dtype=jnp.float32) / half_dim)
    angles = positions.astype(jnp.float32)[:, None, None] * inv_freq
    cos_part = jnp.cos(angles)
    sin_part = jnp.sin(angles)
    lo_half = values[..., :half_dim]
    hi_half = values[..., half_dim:]
    return jnp.concatenate([lo_half * cos_part - hi_half * sin_part, hi_half * cos_part + lo_half * sin_part], axis=-1)


def coords():
    z = lax.axis_index('x')
    p = lax.axis_index('yz')
    core = p % 2
    xx = (p // 2) % 2
    y = p // 4
    partner = p + 1 - 2 * core
    xn = p + 2 - 4 * xx
    yn = p + 4 - 8 * y
    diag = xn + 4 - 8 * y
    z1 = z % 2
    z2 = z // 2
    zs = [z, 2 * z2 + 1 - z1, 2 * (1 - z2) + z1, 3 - z]
    return z, p, core, partner, xn, yn, diag, zs


def entry_signal(z, p, zs):
    sem = pltpu.get_barrier_semaphore()
    for k in range(1, NZ):
        pl.semaphore_signal(sem, inc=1, device_id=(zs[k], p), device_id_type=MESH)
    for k in range(1, NP):
        pl.semaphore_signal(sem, inc=1, device_id=(z, (p + k) % NP), device_id_type=MESH)


def entry_wait():
    pl.semaphore_wait(pltpu.get_barrier_semaphore(), NZ - 1 + NP - 1)


def rcopy(src, dst, send, recv, dev):
    return pltpu.make_async_remote_copy(src_ref=src, dst_ref=dst, send_sem=send, recv_sem=recv, device_id=dev, device_id_type=MESH)


class Relay:
    def __init__(self, z, p, at, whole, send, recv):
        self.z, self.p, self.at, self.whole, self.send, self.recv = z, p, at, whole, send, recv

    def copy(self, way, src, ch, dev):
        ref = self.at(src, ch)
        return rcopy(ref, ref, self.send.at[way], self.recv.at[src, ch], (dev, self.p))

    def inward(self, chunks):
        z = self.z

        @pl.when(z < 2)
        def _():
            for ch in chunks:
                self.copy(0, z, ch, z + 1).start()

        @pl.when(z >= 2)
        def _():
            for ch in chunks:
                self.copy(1, z, ch, z - 1).start()

    def outward(self, chunks):
        z = self.z

        @pl.when(z == 1)
        def _():
            for ch in chunks:
                self.copy(1, z, ch, z - 1).start()

        @pl.when(z == 2)
        def _():
            for ch in chunks:
                self.copy(0, z, ch, z + 1).start()

    def step(self, k, ch):
        z = self.z

        @pl.when(z >= k)
        def _():
            self.copy(0, z - k, ch, z).wait_recv()

            @pl.when(z < 3)
            def _():
                self.copy(2 * k, z - k, ch, z + 1).start()

        @pl.when(z + k <= 3)
        def _():
            self.copy(0, z + k, ch, z).wait_recv()

            @pl.when(z > 0)
            def _():
                self.copy(2 * k + 1, z + k, ch, z - 1).start()

    def sent(self, way):
        rcopy(self.whole, self.whole, self.send.at[way], self.recv.at[0, 0], (self.z, self.p)).wait_send()

    def drain(self):
        z = self.z
        for k in range(NZ - 1):
            @pl.when((z >= k) & (z < 3))
            def _():
                self.sent(2 * k)

            @pl.when((z + k <= 3) & (z > 0))
            def _():
                self.sent(2 * k + 1)


def attn_start(q):
    return pl.multiple_of(64 * q + 16 * (q // 2), 16)


def kernel_a(xT_hbm, ln_hbm, wattn_hbm, w_ref, h_ref, qkv_ref, w1f_ref, w2_ref, ps1_ref, ps2_ref, ps3_ref,
             xg, lng, watt, zsend, zrecv, zq, s1, s2, wn, wt, hT_ref, ln_ref, wattn_ref,
             xsend, xrecv, rpart, lsend, lrecv, asend, arecv, zsend_sem, zrecv_sem, qsend, qrecv, wsend, wrecv, lsem, osem, ldummy):
    z, p, core, partner, xn, yn, diag, zs = coords()
    entry_signal(z, p, zs)
    wload = pltpu.make_async_copy(w_ref, wn, lsem.at[0])
    loads = [
        pltpu.make_async_copy(xT_hbm, xg.at[z, p], lsem.at[6]),
        pltpu.make_async_copy(ln_hbm, ln_ref, lsem.at[7]),
        pltpu.make_async_copy(wattn_hbm, wattn_ref, lsem.at[8]),
        wload,
    ]
    for c in loads:
        c.start()
    lng[z, p] = jnp.zeros((1, 128), F32)
    loads[1].wait()
    lng[z, p, 0:1, 0:64] = ln_ref[...]
    loads[0].wait()
    entry_wait()
    here = (z, p)

    def send(src_z, src_p, dev, way=0):
        recv = rpart.at[0] if way == 4 else xrecv.at[way, src_z]
        rcopy(xg.at[src_z, src_p], xg.at[src_z, src_p], xsend.at[0], recv, dev).start()

    def send_l(src_z, dev, phase):
        rcopy(lng.at[src_z, p], lng.at[src_z, p], lsend.at[0], lrecv.at[phase], dev).start()

    def wait_x(src_z, src_p, way):
        rcopy(xg.at[src_z, src_p], xg.at[src_z, src_p], xsend.at[0], xrecv.at[way, src_z], here).wait_recv()

    def stat(src_z, src_p):
        blk = xg[src_z, src_p].astype(F32).reshape(8, 8, 512)
        s1[...] += jnp.sum(blk, axis=0)
        s2[...] += jnp.sum(blk * blk, axis=0)

    spans = tuple((i, C1A) for i in range(0, C1, C1A))

    def w_piece(i, src, dst, dev):
        o, n = spans[i]
        return rcopy(
            wt.at[:, pl.ds(pl.multiple_of(dst * 256 + o, 16), n), :],
            w1f_ref.at[src, :, pl.ds(o, n), :],
            wsend.at[0], wrecv.at[0], dev)

    def send_w(i):
        for k in (3, 2, 1):
            w_piece(i, z, zs[k], (zs[k], p)).start()

    def turn(odd):
        def body(i, carry):
            lanes = pl.ds(pl.multiple_of(i * 256 + odd * 128, 128), 128)
            blk = wn[:, :, lanes].astype(F32)
            for g in range(2):
                wt[g, lanes, :] = blk[:, g, :].T.astype(BF16)
            return carry

        lax.fori_loop(0, NZ, body, 0)

    mid = 2 - z // 2
    far = 3 - 3 * (z // 2)
    zo = [z, zs[1], mid, far]
    inner = (z == 1) | (z == 2)
    send(z, p, (mid, p))
    send(z, p, (zs[1], p))
    for k in (3, 2, 1):
        send_l(z, (zs[k], p), 0)
    targets = ((diag, 3), (xn, 1), (yn, 2), (partner, 4))
    for dev, way in targets:
        send(z, p, (z, dev), way)
    for j in range(1, NP):
        send_l(z, (z, (p + j) % NP), 1)

    def attn_piece(q):
        return rcopy(wattn_ref.at[pl.ds(attn_start(q), 80), :], watt.at[z], asend.at[0], arecv.at[0], (q, p))

    def outward(k):
        return rcopy(xg.at[zo[k], p], xg.at[zo[k], p], osem.at[k - 2], xrecv.at[0, zo[k]], (zs[1], p))

    s1[...] = jnp.zeros_like(s1)
    s2[...] = jnp.zeros_like(s2)
    stat(z, p)
    loads[2].wait()
    watt[z] = wattn_ref[pl.ds(attn_start(z), 80), :]
    wload.wait()
    turn(0)
    attn_piece(mid).start()

    @pl.when(jnp.logical_not(inner))
    def _():
        attn_piece(zs[1]).start()


    def column(k):
        wait_x(zo[k], p, 0)
        if k >= 2:
            @pl.when(inner)
            def _():
                outward(k).start()
        for dev, way in targets:
            send(zo[k], p, (z, dev), way)
        stat(zo[k], p)

    def pass_on(k, src, way):
        wait_x(zo[k], src, way)
        send(zo[k], src, (z, partner), 4)
        stat(zo[k], src)

    column(1)
    column(2)
    column(3)
    rcopy(ldummy.at[pl.ds(0, 3)], ldummy.at[pl.ds(0, 3)], lsend.at[0], lrecv.at[0], here).wait_recv()
    for k in range(1, NZ):
        for j in range(1, NP):
            send_l(zs[k], (z, (p + j) % NP), 1)
    for k in range(2):
        pass_on(k, xn, 1)
        pass_on(k, yn, 2)
    attn_piece(far).start()

    @pl.when(inner)
    def _():
        attn_piece(zs[1]).start()

    send_w(0)
    pass_on(0, diag, 3)
    pass_on(1, diag, 3)
    for k in range(2, NZ):
        pass_on(k, xn, 1)
        pass_on(k, yn, 2)
        pass_on(k, diag, 3)
    send_w(1)
    half = xg.at[pl.ds(0, 2)]
    rcopy(half, half, xsend.at[0], rpart.at[0], here).wait_recv()
    for q in (partner, partner + xn - p, partner + yn - p, partner + diag - p):
        for k in range(NZ):
            stat(zo[k], q)
    rcopy(ldummy.at[pl.ds(0, 28)], ldummy.at[pl.ds(0, 28)], lsend.at[0], lrecv.at[1], here).wait_recv()

    mean = jnp.sum(s1[...], axis=0, keepdims=True) / 2048.0
    var = jnp.sum(s2[...], axis=0, keepdims=True) / 2048.0 - mean * mean
    rstd = lax.rsqrt(var + LN_EPS)
    lnT = jnp.concatenate([lng[i // NP, i % NP, 0:1, :] for i in range(32)] + [jnp.zeros((96, 128), F32)], axis=0).T
    for i in range(NZ * NP):
        sc = lnT[0:64, i:i + 1]
        hT_ref[i * 64:(i + 1) * 64, :] = ((xg[i // NP, i % NP].astype(F32) - mean) * rstd * sc).astype(BF16)

    hout = pltpu.make_async_copy(hT_ref, h_ref, lsem.at[5])
    hout.start()
    three = watt.at[pl.ds(0, 3)]
    rcopy(three, three, asend.at[0], arecv.at[0], here).wait_recv()
    part = None
    for q in range(NZ):
        t = jnp.dot(watt[q], hT_ref[q * 512:(q + 1) * 512, :], preferred_element_type=F32)
        part = t if part is None else part + t
    part = part.astype(BF16)
    for q in range(NZ):
        zsend[q] = part[:, q * 128:(q + 1) * 128]
    for k in (3, 2, 1):
        rcopy(zsend.at[zs[k]], zrecv.at[z], zsend_sem.at[0], zrecv_sem.at[0], (zs[k], p)).start()
    zrecv[z] = zsend[z]
    turn(1)
    send_w(2)
    outs = [pltpu.make_async_copy(wt, w2_ref, lsem.at[1])]
    for i, ps_ref in enumerate((ps1_ref, ps2_ref, ps3_ref)):
        dst = (z + i + 1) % NZ
        outs.append(pltpu.make_async_copy(wt.at[:, pl.ds(pl.multiple_of(dst * 256 + C1, 16), C2), :], ps_ref, lsem.at[2 + i]))
    for c in outs[1:] + outs[:1]:
        c.start()
    zthree = rcopy(zsend.at[pl.ds(0, 3)], zrecv.at[pl.ds(0, 3)], zsend_sem.at[0], zrecv_sem.at[0], here)
    zthree.wait_recv()
    zt = jnp.concatenate([zrecv[0].astype(F32), zrecv[1].astype(F32)[16:80], zrecv[2].astype(F32), zrecv[3].astype(F32)[16:80]], axis=0)
    zq[...] = zt.T.astype(BF16).reshape(NP, 16, 288)
    for j in range(1, NP):
        q = (p + j) % NP
        rcopy(zq.at[q], qkv_ref.at[p], qsend.at[0], qrecv.at[0], (z, q)).start()
    qown = pltpu.make_async_copy(zq.at[p], qkv_ref.at[p], lsem.at[9])
    qown.start()
    qseven = rcopy(zq.at[pl.ds(0, 7)], qkv_ref.at[pl.ds(0, 7)], qsend.at[0], qrecv.at[0], here)
    qseven.wait_recv()
    wthree = w1f_ref.at[pl.ds(0, 3)]
    wall = rcopy(wthree, wthree, wsend.at[0], wrecv.at[0], here)
    wall.wait_recv()
    hout.wait()
    qown.wait()
    for c in outs:
        c.wait()
    sent30 = w2_ref.at[:, pl.ds(0, 960), :]
    rcopy(sent30, sent30, xsend.at[0], rpart.at[0], here).wait_send()
    rcopy(ldummy, ldummy, lsend.at[0], lrecv.at[0], here).wait_send()
    rcopy(three, three, asend.at[0], arecv.at[0], here).wait_send()
    zthree.wait_send()
    qseven.wait_send()
    wall.wait_send()

    @pl.when(inner)
    def _():
        outward(2).wait_send()
        outward(3).wait_send()


def call_a(xT, ln, wattnT, w):
    hbm = pl.BlockSpec(memory_space=pl.ANY)
    return pl.pallas_call(
        kernel_a,
        out_shape=(
            jax.ShapeDtypeStruct((2048, 512), BF16),
            jax.ShapeDtypeStruct((NP, 16, 288), BF16),
            jax.ShapeDtypeStruct((NZ, 2, C1, 512), BF16),
            jax.ShapeDtypeStruct((2, 1024, 512), BF16),
        ) + (jax.ShapeDtypeStruct((2, C2, 512), BF16),) * 3,
        in_specs=[hbm] * 4,
        out_specs=(hbm,) * 7,
        scratch_shapes=[
            pltpu.VMEM((NZ, NP, 64, 512), BF16),
            pltpu.VMEM((NZ, NP, 1, 128), F32),
            pltpu.VMEM((NZ, 80, 512), BF16),
            pltpu.VMEM((NZ, 80, 128), BF16),
            pltpu.VMEM((NZ, 80, 128), BF16),
            pltpu.VMEM((NP, 16, 288), BF16),
            pltpu.VMEM((8, 512), F32),
            pltpu.VMEM((8, 512), F32),
            pltpu.VMEM((512, 2, 1024), BF16),
            pltpu.VMEM((2, 1024, 512), BF16),
            pltpu.VMEM((2048, 512), BF16),
            pltpu.VMEM((1, 64), F32),
            pltpu.VMEM((288, 512), BF16),
            pltpu.SemaphoreType.DMA((1,)),
            pltpu.SemaphoreType.DMA((4, NZ)),
            pltpu.SemaphoreType.DMA((1,)),
            pltpu.SemaphoreType.DMA((1,)),
            pltpu.SemaphoreType.DMA((2,)),
            pltpu.SemaphoreType.DMA((1,)),
            pltpu.SemaphoreType.DMA((1,)),
            pltpu.SemaphoreType.DMA((1,)),
            pltpu.SemaphoreType.DMA((1,)),
            pltpu.SemaphoreType.DMA((1,)),
            pltpu.SemaphoreType.DMA((1,)),
            pltpu.SemaphoreType.DMA((1,)),
            pltpu.SemaphoreType.DMA((1,)),
            pltpu.SemaphoreType.DMA((10,)),
            pltpu.SemaphoreType.DMA((2,)),
            pltpu.VMEM((31, 1, 128), F32),
        ],
        compiler_params=pltpu.CompilerParams(collective_id=0, has_side_effects=True, vmem_limit_bytes=56 * 1024 * 1024),
        name='gather_norm_qkv',
    )(xT, ln, wattnT, w)


def kernel_b(len_ref, q_ref, k_ref, v_ref, kc_ref, vc_ref, o_ref, kn_ref, vn_ref, kbuf, vbuf, oscr, isem, osem):
    rows = kbuf.shape[0]
    seq = kbuf.shape[1]

    def load(b, t):
        return pltpu.make_async_copy((kc_ref, vc_ref)[t].at[b], (kbuf, vbuf)[t].at[b], isem.at[b])

    def store(b, t):
        return pltpu.make_async_copy((kbuf, vbuf)[t].at[b], (kn_ref, vn_ref)[t].at[b], osem.at[0])

    for b in range(rows):
        load(b, 0).start()
        load(b, 1).start()

    def insert(buf, b, length, new):
        base = pl.multiple_of((length // 16) * 16, 16)
        hit = base + lax.broadcasted_iota(jnp.int32, (16, 128), 0) == length
        buf[b, pl.ds(base, 16), :] = jnp.where(hit, new.astype(F32), buf[b, pl.ds(base, 16), :].astype(F32)).astype(BF16)

    def attend(b, length, n):
        scores = lax.dot_general(q_ref[b], kbuf[b, 0:n, :], (((1,), (1,)), ((), ())), preferred_element_type=F32) * (128.0 ** -0.5)
        slot = lax.broadcasted_iota(jnp.int32, scores.shape, 1)
        scores = jnp.where(slot <= length, scores, -1e30)
        top = jnp.max(scores, axis=1, keepdims=True)
        e = jnp.exp(scores - top)
        probs = (e / jnp.sum(e, axis=1, keepdims=True)).astype(BF16)
        return jnp.dot(probs, vbuf[b, 0:n, :], preferred_element_type=F32)

    def pair(i, carry):
        b0 = 2 * i
        b1 = 2 * i + 1
        l0 = len_ref[b0]
        l1 = len_ref[b1]
        for b, length in ((b0, l0), (b1, l1)):
            pltpu.make_async_copy(kc_ref.at[pl.ds(0, 2)], kbuf.at[pl.ds(0, 2)], isem.at[b]).wait()
            insert(kbuf, b, length, k_ref[b])
            insert(vbuf, b, length, v_ref[b])
        last = jnp.maximum(l0, l1) // 512
        for t in range(seq // 512):
            @pl.when(last == t)
            def _():
                n = 512 * (t + 1)
                r0 = attend(b0, l0, n)
                r1 = attend(b1, l1, n)
                oscr[b0] = r0
                oscr[b1] = r1
        for b in (b0, b1):
            store(b, 0).start()
            store(b, 1).start()
        return carry

    lax.fori_loop(0, rows // 2, pair, 0)
    for h in range(16):
        o_ref[h // 2, :, (h % 2) * 128:(h % 2 + 1) * 128] = oscr[:, h, :].astype(BF16)
    pltpu.make_async_copy(kbuf, kn_ref, osem.at[0]).wait()
    pltpu.make_async_copy(vbuf, vn_ref, osem.at[0]).wait()


def call_b(lengths, q_rot, k_rot, v_tok, k_cache, v_cache):
    rows, seq, hd = k_cache.shape
    heads = q_rot.shape[1]
    vm = pl.BlockSpec(memory_space=pltpu.VMEM)
    hbm = pl.BlockSpec(memory_space=pl.ANY)
    return pl.pallas_call(
        kernel_b,
        in_specs=[pl.BlockSpec(memory_space=pltpu.SMEM), vm, vm, vm, hbm, hbm],
        out_specs=(vm, hbm, hbm),
        out_shape=(
            jax.ShapeDtypeStruct((NP, rows, heads * hd // NP), BF16),
            jax.ShapeDtypeStruct(k_cache.shape, BF16),
            jax.ShapeDtypeStruct(v_cache.shape, BF16),
        ),
        scratch_shapes=[
            pltpu.VMEM((rows, seq, hd), BF16),
            pltpu.VMEM((rows, seq, hd), BF16),
            pltpu.VMEM((rows, heads, hd), F32),
            pltpu.SemaphoreType.DMA((rows,)),
            pltpu.SemaphoreType.DMA((1,)),
        ],
        compiler_params=pltpu.CompilerParams(vmem_limit_bytes=58 * 1024 * 1024),
        cost_estimate=pl.CostEstimate(flops=12_000_000_000, bytes_accessed=33_000_000, transcendentals=0),
        name='attend',
    )(lengths, q_rot, k_rot, v_tok, k_cache, v_cache)


def kernel_c(hT, w2_ref, w1f_ref, p1_ref, p2_ref, p3_ref, wd, wo, o_ref, xT_ref, y_ref,
             wvA, wvB, wdAT, wdBT, woT, og, hidA, hidB, yA, ysum, r1, acc, r2,
             wsem, wbsend, wbrecv, osend, orecv, gsend, grecv, hasend, harecv, hbsend, hbrecv,
             r1send, r1recv, r2send, r2recv):
    z, p, core, partner, xn, yn, diag, zs = coords()
    entry_signal(z, p, zs)
    local = [pltpu.make_async_copy(w2_ref.at[:, pl.ds(pl.multiple_of(z * 256, 256), CA), :], wvA.at[z], wsem.at[0])]
    for s, p_ref in ((1, p1_ref), (2, p2_ref), (3, p3_ref)):
        src = (z + NZ - s) % NZ
        local.append(pltpu.make_async_copy(w1f_ref.at[src], wvA.at[src, :, pl.ds(0, C1), :], wsem.at[0]))
        local.append(pltpu.make_async_copy(p_ref, wvA.at[src, :, pl.ds(C1, C2), :], wsem.at[0]))
    late = [
        pltpu.make_async_copy(w2_ref.at[:, pl.ds(pl.multiple_of(z * 256 + CA, 16), C3), :], wvB.at[z], wsem.at[1]),
    ]
    for c in local + late:
        c.start()
    entry_wait()
    here = (z, p)

    def w_piece(src, dst, dev):
        return rcopy(
            w2_ref.at[:, pl.ds(pl.multiple_of(dst * 256 + CA, 16), C3), :],
            wvB.at[src], wbsend.at[0], wbrecv.at[0], dev)

    for k in (3, 2, 1):
        w_piece(z, zs[k], (zs[k], p)).start()
    for j in range(1, NP):
        q = (p + j) % NP
        rcopy(o_ref.at[q], og.at[z, p], osend.at[0], orecv.at[0], (z, q)).start()
    og[z, p] = o_ref[p]

    def gated(wv, n):
        g = None
        for q in range(NZ):
            t = jnp.dot(wv[q].reshape(2 * n, 512), hT[q * 512:(q + 1) * 512, :], preferred_element_type=F32)
            g = t if g is None else g + t
        gate = g[0:n].astype(BF16).astype(F32)
        up = g[n:2 * n].astype(BF16).astype(F32)
        return (jax.nn.silu(gate) * up).astype(BF16)

    ra = Relay(z, p, lambda src, ch: hidA.at[ch, src], hidA.at[0], hasend, harecv)
    rb = Relay(z, p, lambda src, ch: hidB.at[ch, src], hidB.at[0], hbsend, hbrecv)
    ro = Relay(z, p, lambda src, ch: og.at[src], og.at[0], gsend, grecv)
    every = range(CHUNKS)

    pltpu.make_async_copy(wvA, wvA, wsem.at[0]).wait()
    ha = gated(wvA, CA)
    for ch in every:
        hidA[ch, z] = ha[:, ch * LANES:(ch + 1) * LANES]

    ra.outward(every)
    ra.inward(range(2))
    oseven = rcopy(o_ref.at[pl.ds(0, 7)], og.at[z, pl.ds(0, 7)], osend.at[0], orecv.at[0], here)
    oseven.wait_recv()
    ro.outward(range(1))
    ro.inward(range(1))
    for c in late:
        c.wait()
    def by_core(ref, w):
        w = w.T.reshape(4, 2, 64, w.shape[0])
        for j in range(2):
            ref[j] = w[:, j].reshape(256, w.shape[3])

    by_core(wdAT, jnp.concatenate([wd[q * 256:q * 256 + CA, :] for q in range(NZ)], axis=0))
    by_core(wdBT, jnp.concatenate([wd[q * 256 + CA:(q + 1) * 256, :] for q in range(NZ)], axis=0))
    by_core(woT, wo[...])

    wthree = wvB.at[pl.ds(0, 3)]
    wall = rcopy(wthree, wthree, wbsend.at[0], wbrecv.at[0], here)
    wall.wait_recv()
    hb = gated(wvB, C3)
    for ch in range(CHUNKS):
        hidB[ch, z] = hb[:, ch * LANES:(ch + 1) * LANES]
    rb.outward(every)
    rb.inward(range(2))
    for ch in range(2, CHUNKS):
        ra.inward((ch,))
        rb.inward((ch,))
    ro.step(1, 0)
    for ch in range(2):
        ra.step(1, ch)
    for ch in range(2):
        ra.step(2, ch)

    chip = p // 2
    others = [diag // 2, xn // 2, yn // 2]

    def d2d(ch):
        return rcopy(ysum.at[ch, 1 - core], r1.at[ch], r1send.at[0], r1recv.at[ch], (z, partner))

    def hop(ch, i, dev):
        return rcopy(acc.at[ch, i], r2.at[ch, i], r2send.at[0], r2recv.at[ch], (z, dev))

    def stage0(ch):
        o_rows = og[ch * NZ // CHUNKS].reshape(128, 256)
        for j in (1 - core, core):
            yA[j] = jnp.dot(wdAT[j], hidA[ch].reshape(NZ * CA, LANES), preferred_element_type=F32) + lax.dot_general(
                woT[j], o_rows, (((1,), (1,)), ((), ())), preferred_element_type=F32)

    def half(ch, j):
        yt = yA[j] + jnp.dot(wdBT[j], hidB[ch].reshape(NZ * C3, LANES), preferred_element_type=F32)
        ysum[ch, j] = yt.reshape(4, 64, LANES)

    def stage1(ch):
        half(ch, 1 - core)
        d2d(ch).start()
        half(ch, core)

    def stage2(ch):
        d2d(ch).wait_recv()
        for i, (t, dev) in enumerate(zip(others, (diag, xn, yn))):
            acc[ch, i] = ysum[ch, core, t] + r1[ch, t]
            hop(ch, i, dev).start()

    def stage3(ch):
        lanes = slice(ch * LANES, (ch + 1) * LANES)
        mine = ysum[ch, core, chip] + r1[ch, chip]
        rcopy(acc.at[ch], r2.at[ch], r2send.at[0], r2recv.at[ch], here).wait_recv()
        for i in range(3):
            mine = mine + r2[ch, i]
        y_ref[:, lanes] = (xT_ref[:, lanes].astype(F32) + mine).astype(BF16)

    for t in range(1, CHUNKS + 3):
        for k in range(1, NZ - 1):
            ch = t - k
            if 0 <= ch < CHUNKS:
                if ch >= 2:
                    ra.step(k, ch)
                rb.step(k, ch)
        if t < 3:
            ro.step(t + 1, 0)
        if t >= 3:
            ra.step(3, t - 3)
            stage0(t - 3)
            rb.step(3, t - 3)
            stage1(t - 3)
        if t >= 4:
            stage2(t - 4)
    stage2(CHUNKS - 1)
    for ch in every:
        stage3(ch)

    wall.wait_send()
    oseven.wait_send()
    rcopy(r1, r1, r1send.at[0], r1recv.at[0], here).wait_send()
    rcopy(acc, acc, r2send.at[0], r2recv.at[0], here).wait_send()
    ra.drain()
    rb.drain()
    ro.drain()


def call_c(hT, w2, w1f, ps, wd, wo, o8, xT):
    vm = pl.BlockSpec(memory_space=pltpu.VMEM)
    hbm = pl.BlockSpec(memory_space=pl.ANY)
    return pl.pallas_call(
        kernel_c,
        out_shape=jax.ShapeDtypeStruct((64, 512), BF16),
        in_specs=[vm] + [hbm] * 5 + [vm] * 4,
        out_specs=vm,
        scratch_shapes=[
            pltpu.VMEM((NZ, 2, CA, 512), BF16),
            pltpu.VMEM((NZ, 2, C3, 512), BF16),
            pltpu.VMEM((2, 256, NZ * CA), BF16),
            pltpu.VMEM((2, 256, NZ * C3), BF16),
            pltpu.VMEM((2, 256, 256), BF16),
            pltpu.VMEM((NZ, NP, 16, 256), BF16),
            pltpu.VMEM((CHUNKS, NZ, CA, LANES), BF16),
            pltpu.VMEM((CHUNKS, NZ, C3, LANES), BF16),
            pltpu.VMEM((2, 256, LANES), F32),
            pltpu.VMEM((CHUNKS, 2, 4, 64, LANES), F32),
            pltpu.VMEM((CHUNKS, 4, 64, LANES), F32),
            pltpu.VMEM((CHUNKS, 3, 64, LANES), F32),
            pltpu.VMEM((CHUNKS, 3, 64, LANES), F32),
            pltpu.SemaphoreType.DMA((2,)),
            pltpu.SemaphoreType.DMA((1,)),
            pltpu.SemaphoreType.DMA((1,)),
            pltpu.SemaphoreType.DMA((1,)),
            pltpu.SemaphoreType.DMA((1,)),
            pltpu.SemaphoreType.DMA((6,)),
            pltpu.SemaphoreType.DMA((NZ, 1)),
            pltpu.SemaphoreType.DMA((6,)),
            pltpu.SemaphoreType.DMA((NZ, CHUNKS)),
            pltpu.SemaphoreType.DMA((6,)),
            pltpu.SemaphoreType.DMA((NZ, CHUNKS)),
            pltpu.SemaphoreType.DMA((1,)),
            pltpu.SemaphoreType.DMA((CHUNKS,)),
            pltpu.SemaphoreType.DMA((1,)),
            pltpu.SemaphoreType.DMA((CHUNKS,)),
        ],
        compiler_params=pltpu.CompilerParams(collective_id=1, has_side_effects=True, vmem_limit_bytes=40 * 1024 * 1024),
        cost_estimate=pl.CostEstimate(flops=12_000_000_000, bytes_accessed=6_000_000, transcendentals=0),
        name='mlp_out',
    )(hT, w2, w1f, *ps, wd, wo, o8, xT)


def solution(mesh):
    all_axes = ('x', 'yz')

    def local_step(x_in, ln_scale, w_gate_up, w_attn, w_down, w_out, k_cache, v_cache, lengths, positions):
        xT = x_in.T
        wattnT = w_attn.T
        hT, qkv, w1f, w2, *pieces = call_a(xT, ln_scale[None, :], wattnT, w_gate_up)
        ps = [lax.ppermute(pieces[i], 'x', [(q, (q + i + 1) % NZ) for q in range(NZ)]) for i in range(NZ - 1)]
        proj = jnp.transpose(qkv, (1, 0, 2)).reshape(16, 2304)
        q_raw = proj[:, :2048].reshape(16, 16, 128)
        k_tok = proj[:, 2048:2176]
        v_tok = proj[:, 2176:]
        q_rot = rotary(q_raw.astype(F32), positions).astype(BF16)
        k_rot = rotary(k_tok[:, None, :].astype(F32), positions).astype(BF16)
        o8, k_new, v_new = call_b(lengths, q_rot, k_rot, v_tok[:, None, :], k_cache, v_cache)
        yT = call_c(hT, w2, w1f, ps, w_down, w_out, o8, xT)
        return yT.T, k_new, v_new

    row_spec = P(None, all_axes)
    vec_spec = P(all_axes)
    cache_spec = P(all_axes, None, None)
    return jax.shard_map(
        local_step,
        mesh=mesh,
        in_specs=(row_spec, vec_spec, P('x', None, 'yz'), P('x', 'yz'), P('yz', 'x'), P('yz', 'x'), cache_spec, cache_spec, vec_spec, vec_spec),
        out_specs=(row_spec, cache_spec, cache_spec),
        check_vma=False,
    )
```

profile of v0, /device:TPU:0, one launch (start us, length us, event | category | flops | bytes accessed | tf_op | source)
XLA Modules:
  0.0 104.3 jit_solution(17330636766716160279)
XLA Ops:
  0.6 30.7 %gather_norm_qkv.1 = (bf16[2048,512]{1,0:T(8,128)(2,1)}, bf16[8,16,288]{2,1,0:T(8,128)(2,1)}, bf16[4,2,48,512]{3,2,1,0:T(8,128)(2,1)}, bf16[2,1024,512]{2,1,0:T(...) custom-call(bf16[64,512]{1,0:T(8,128)(2,1)} %bitcast.12, ...), custom_call_target="tpu_custom_call" | custom-call | tf_op jit(solution)/shard_map/gather_norm_qkv/pallas_call | solution.py:345
  31.3 1.4 %collective-permute-start = (bf16[2,128,512]{2,1,0:T(8,128)(2,1)}, bf16[2,128,512]{2,1,0:T(8,128)(2,1)S(1)}, u32[]{:S(2)}, u32[]{:S(2)}) collective-permute-start(bf16[2,128,512]{2,1,0:T(8,128)(2,1)} %get-tuple-element.16), channel_id=1, source_target_pairs={{0,8},{8,16},{16,24},{24,0},{1,9},{9,17},{17,25},{25,1},{2,10},{10... | collective-permute-start | bytes 786440 | tf_op jit(solution)/shard_map/ppermute | solution.py:678
  32.7 2.3 %collective-permute-start.1 = (bf16[2,128,512]{2,1,0:T(8,128)(2,1)}, bf16[2,128,512]{2,1,0:T(8,128)(2,1)}, u32[]{:S(2)}, u32[]{:S(2)}) collective-permute-start(bf16[2,128,512]{2,1,0:T(8,128)(2,1)} %get-tuple-element.17), channel_id=1, source_target_pairs={{0,16},{8,24},{16,0},{24,8},{1,17},{9,25},{17,1},{25,9},{2,18},{10... | collective-permute-start | bytes 786440 | tf_op jit(solution)/shard_map/ppermute | solution.py:678
  35.0 0.9 collective-permute-start.2
  35.9 0.9 copy.17
  36.8 0.1 reshape.148
  36.9 0.7 convert_element_type.20
  37.6 0.6 copy.19.v_ref
  38.2 0.1 multiply_cosine_fusion
  38.4 0.1 mul.89
  38.4 0.3 subtract_convert_fusion.1
  38.7 0.7 pad_maximum_fusion.1.k_ref
  39.4 0.1 subtract_convert_fusion
  39.5 0.7 pad_maximum_fusion.q_ref
  40.2 0.0 copy-start.4
  40.2 0.0 copy-start.5
  40.2 14.7 %attend.1 = (bf16[8,16,256]{2,1,0:T(8,128)(2,1)}, bf16[16,2048,128]{2,1,0:T(8,128)(2,1)}, bf16[16,2048,128]{2,1,0:T(8,128)(2,1)}) custom-call(s32[16]{0:T(128)} %len_ref.1, bf16[16,16,128]{2,1,0:T(8,128)(2,1)} %pad_maximum_fusion.q_ref, bf16[16,1,128]{2,1,0:T(2,128)(2,1)} %pad_maximum_fusion.1.k_ref, bf16[16,1,128]{2,1,0:T(2,128)(2,1)} %copy.19.v_ref, ...), custom_call_target="tpu_custom_call" | custom-call | flops 12000000000 | bytes 33000000 | tf_op jit(solution)/shard_map/attend/pallas_call | solution.py:454
  55.0 0.0 collective-permute-done.p1_ref
  55.0 0.0 collective-permute-done.1.p2_ref
  55.0 0.0 collective-permute-done.2.p3_ref
  55.0 0.0 copy-done
  55.1 0.8 copy-done.6
  55.9 47.7 %mlp_out.1 = bf16[64,512]{1,0:T(8,128)(2,1)S(1)} custom-call(bf16[2048,512]{1,0:T(8,128)(2,1)S(1)} %copy-done.1, bf16[2,1024,512]{2,1,0:T(8,128)(2,1)S(1)} %copy-done.2, bf16[4,2,48,512]{3,2,1,0:T(8,128)(2,1)S(1)} %copy-done.4, bf16[2,128,512]{2,1,0:T(8,128)(2,1)S(1)} %collective-permute-done.p1_ref, bf16[2,128,512]{2,1,0:T(8,128)(2,1)} %collective-permute-done.1.p2_ref, ...), custom_call_target="tpu_custom_call" | custom-call | flops 12000000000 | bytes 6000000 | tf_op jit(solution)/shard_map/mlp_out/pallas_call | solution.py:630
  103.6 0.6 copy.22
  (14 shorter events, 0.1 us)
Async XLA Ops:
  31.3 23.7 %collective-permute-start = (bf16[2,128,512]{2,1,0:T(8,128)(2,1)}, bf16[2,128,512]{2,1,0:T(8,128)(2,1)S(1)}, u32[]{:S(2)}, u32[]{:S(2)}) collective-permute-start(bf16[2,128,512]{2,1,0:T(8,128)(2,1)} %get-tuple-element.16), channel_id=1, source_target_pairs={{0,8},{8,16},{16,24},{24,0},{1,9},{9,17},{17,25},{25,1},{2,10},{10... | collective-permute-start | bytes 786440 | tf_op jit(solution)/shard_map/ppermute | solution.py:678
  32.7 22.3 %collective-permute-start.1 = (bf16[2,128,512]{2,1,0:T(8,128)(2,1)}, bf16[2,128,512]{2,1,0:T(8,128)(2,1)}, u32[]{:S(2)}, u32[]{:S(2)}) collective-permute-start(bf16[2,128,512]{2,1,0:T(8,128)(2,1)} %get-tuple-element.17), channel_id=1, source_target_pairs={{0,16},{8,24},{16,0},{24,8},{1,17},{9,25},{17,1},{25,9},{2,18},{10... | collective-permute-start | bytes 786440 | tf_op jit(solution)/shard_map/ppermute | solution.py:678
  35.0 20.0 %collective-permute-start.2 = (bf16[2,128,512]{2,1,0:T(8,128)(2,1)}, bf16[2,128,512]{2,1,0:T(8,128)(2,1)}, u32[]{:S(2)}, u32[]{:S(2)}) collective-permute-start(bf16[2,128,512]{2,1,0:T(8,128)(2,1)} %get-tuple-element.18), channel_id=1, source_target_pairs={{0,24},{8,0},{16,8},{24,16},{1,25},{9,1},{17,9},{25,17},{2,26},{10... | collective-permute-start | bytes 786440 | tf_op jit(solution)/shard_map/ppermute | solution.py:678
  40.2 14.8 %copy-start = (bf16[512,64]{0,1:T(8,128)(2,1)S(1)}, bf16[512,64]{0,1:T(8,128)(2,1)}, u32[]{:S(2)}) copy-start(bf16[512,64]{0,1:T(8,128)(2,1)} %param.10) | copy-start | bytes 196612
  40.2 14.8 %copy-start.1 = (bf16[2048,512]{1,0:T(8,128)(2,1)S(1)}, bf16[2048,512]{1,0:T(8,128)(2,1)}, u32[]{:S(2)}) copy-start(bf16[2048,512]{1,0:T(8,128)(2,1)} %get-tuple-element.13.hT) | copy-start | bytes 6291460
  40.2 14.8 %copy-start.2 = (bf16[2,1024,512]{2,1,0:T(8,128)(2,1)S(1)}, bf16[2,1024,512]{2,1,0:T(8,128)(2,1)}, u32[]{:S(2)}) copy-start(bf16[2,1024,512]{2,1,0:T(8,128)(2,1)} %get-tuple-element.14.w2_ref) | copy-start | bytes 6291460
  40.2 14.8 %copy-start.3 = (bf16[1024,512]{1,0:T(8,128)(2,1)S(1)}, bf16[1024,512]{1,0:T(8,128)(2,1)}, u32[]{:S(2)}) copy-start(bf16[1024,512]{1,0:T(8,128)(2,1)} %wd.1) | copy-start | bytes 3145732
  40.2 14.8 %copy-start.4 = (bf16[4,2,48,512]{3,2,1,0:T(8,128)(2,1)S(1)}, bf16[4,2,48,512]{3,2,1,0:T(8,128)(2,1)}, u32[]{:S(2)}) copy-start(bf16[4,2,48,512]{3,2,1,0:T(8,128)(2,1)} %get-tuple-element.15.w1f_ref) | copy-start | bytes 1179652
  40.2 14.8 %copy-start.5 = (bf16[256,512]{1,0:T(8,128)(2,1)S(1)}, bf16[256,512]{1,0:T(8,128)(2,1)}, u32[]{:S(2)}) copy-start(bf16[256,512]{1,0:T(8,128)(2,1)} %wo.1) | copy-start | bytes 786436
  55.1 0.8 copy-start.6
where the time goes:
time: 104 us
  Pallas kernels  93.1 us (90%)
  starting transfers between devices  4.54 us (4%)
  local copies, waits for them, and re-layouts  3.23 us (3%)
  other arithmetic  2.58 us (2%)
    pallas_call x1, Pallas kernels, call_c(): pl.pallas_call(kernel_c, out_shape=jax.ShapeDtypeStruct((64, 512), BF16),...  47.7 us
    pallas_call x1, Pallas kernels, call_a(): pl.pallas_call(kernel_a, out_shape=(jax.ShapeDtypeStruct((2048, 512), BF1...  30.7 us
    pallas_call x1, Pallas kernels, call_b(): pl.pallas_call(kernel_b, in_specs=[pl.BlockSpec(memory_space=pltpu.SMEM),...  14.7 us
    ppermute x3, starting transfers between devices, local_step(): lax.ppermute(pieces[i], 'x', [(q, (q + i + 1) % NZ) for q in range(NZ)])  4.54 us
  transfers between devices with their start and end apart: 3, of which 0 were waited for; matrix products, arithmetic and copies ran while one was open for 4% of the time, Pallas kernels for 14%

commit v1 on v0

--- a/solution.py
+++ b/solution.py
@@ -467,7 +467,7 @@
             pltpu.SemaphoreType.DMA((rows,)),
             pltpu.SemaphoreType.DMA((1,)),
         ],
-        compiler_params=pltpu.CompilerParams(vmem_limit_bytes=58 * 1024 * 1024),
+        compiler_params=pltpu.CompilerParams(vmem_limit_bytes=52 * 1024 * 1024),
         cost_estimate=pl.CostEstimate(flops=12_000_000_000, bytes_accessed=33_000_000, transcendentals=0),
         name='attend',
     )(lengths, q_rot, k_rot, v_tok, k_cache, v_cache)

time: 104 us -> 104 us (level)
  other arithmetic: 2.58 us -> 1.35 us
    pallas_call x1, Pallas kernels: 47.7 us -> 49.8 us  [call_c(): pl.pallas_call(kernel_c, out_shape=jax.ShapeDtypeStruct((64, 512), BF16),...]
    pallas_call x1, Pallas kernels: 14.7 us -> 13.3 us  [call_b(): pl.pallas_call(kernel_b, in_specs=[pl.BlockSpec(memory_space=pltpu.SMEM),...]
    concatenate x2, other arithmetic: 1.41 us -> 0.18 us  [rotary(): jnp.concatenate([lo_half * cos_part - hi_half * sin_part, hi_half * cos_p...]
  transfers between devices with their start and end apart: 3 -> 3, of which waited for: 0 -> 1; matrix products, arithmetic and copies ran while one was open for 4% -> 2% of each run, Pallas kernels for 14% -> 13%
where the time goes in v1:
time: 104 us; the launch traced here: 103 us
  Pallas kernels  93.8 us (90%)
  starting transfers between devices  4.54 us (4%)
  local copies, waits for them, and re-layouts  2.45 us (2%)
  other arithmetic  1.35 us (1%)
    pallas_call x1, Pallas kernels, call_c(): pl.pallas_call(kernel_c, out_shape=jax.ShapeDtypeStruct((64, 512), BF16),...  49.8 us
    pallas_call x1, Pallas kernels, call_a(): pl.pallas_call(kernel_a, out_shape=(jax.ShapeDtypeStruct((2048, 512), BF1...  30.7 us
    pallas_call x1, Pallas kernels, call_b(): pl.pallas_call(kernel_b, in_specs=[pl.BlockSpec(memory_space=pltpu.SMEM),...  13.3 us
    ppermute x3, starting transfers between devices, local_step(): lax.ppermute(pieces[i], 'x', [(q, (q + i + 1) % NZ) for q in range(NZ)])  4.54 us
  transfers between devices with their start and end apart: 3, of which 1 were waited for; matrix products, arithmetic and copies ran while one was open for 2% of the time, Pallas kernels for 13%

profile of v1, /device:TPU:0, one launch (start us, length us, event | category | flops | bytes accessed | tf_op | source)
XLA Modules:
  0.0 103.4 jit_solution(11402091151085478796)
XLA Ops:
  0.6 30.7 %gather_norm_qkv.1 = (bf16[2048,512]{1,0:T(8,128)(2,1)}, bf16[8,16,288]{2,1,0:T(8,128)(2,1)}, bf16[4,2,48,512]{3,2,1,0:T(8,128)(2,1)}, bf16[2,1024,512]{2,1,0:T(...) custom-call(bf16[64,512]{1,0:T(8,128)(2,1)} %bitcast.12, ...), custom_call_target="tpu_custom_call" | custom-call | tf_op jit(solution)/shard_map/gather_norm_qkv/pallas_call | solution.py:345
  31.3 1.4 %collective-permute-start = (bf16[2,128,512]{2,1,0:T(8,128)(2,1)}, bf16[2,128,512]{2,1,0:T(8,128)(2,1)S(1)}, u32[]{:S(2)}, u32[]{:S(2)}) collective-permute-start(bf16[2,128,512]{2,1,0:T(8,128)(2,1)} %get-tuple-element.16), channel_id=1, source_target_pairs={{0,8},{8,16},{16,24},{24,0},{1,9},{9,17},{17,25},{25,1},{2,10},{10... | collective-permute-start | bytes 786440 | tf_op jit(solution)/shard_map/ppermute | solution.py:678
  32.7 2.3 %collective-permute-start.1 = (bf16[2,128,512]{2,1,0:T(8,128)(2,1)}, bf16[2,128,512]{2,1,0:T(8,128)(2,1)S(1)}, u32[]{:S(2)}, u32[]{:S(2)}) collective-permute-start(bf16[2,128,512]{2,1,0:T(8,128)(2,1)} %get-tuple-element.17), channel_id=1, source_target_pairs={{0,16},{8,24},{16,0},{24,8},{1,17},{9,25},{17,1},{25,9},{2,18},{10... | collective-permute-start | bytes 786440 | tf_op jit(solution)/shard_map/ppermute | solution.py:678
  35.0 0.9 collective-permute-start.2
  35.9 0.9 copy.17
  36.8 0.1 reshape.148
  36.9 0.7 convert_element_type.20
  37.6 0.1 multiply_cosine_fusion
  37.8 0.1 mul.89
  37.8 0.3 subtract_convert_fusion.1
  38.1 0.1 pad_maximum_fusion.1.k_ref
  38.2 0.1 subtract_convert_fusion
  38.3 0.1 pad_maximum_fusion.q_ref
  38.4 0.0 copy-start.6
  38.4 0.6 copy-done.6
  39.1 0.0 copy-start.5
  39.1 13.3 %attend.1 = (bf16[8,16,256]{2,1,0:T(8,128)(2,1)S(1)}, bf16[16,2048,128]{2,1,0:T(8,128)(2,1)}, bf16[16,2048,128]{2,1,0:T(8,128)(2,1)}) custom-call(s32[16]{0:T(128)S(1)} %copy-done.6, bf16[16,16,128]{2,1,0:T(8,128)(2,1)S(1)} %pad_maximum_fusion.q_ref, bf16[16,1,128]{2,1,0:T(2,128)(2,1)S(1)} %pad_maximum_fusion.1.k_ref, bf16[16,1,128]{2,1,0:T(2,128)(2,1)S(1)} %copy.19.v_ref, ...), custom_call_target="tpu_custom_call" | custom-call | flops 12000000000 | bytes 33000000 | tf_op jit(solution)/shard_map/attend/pallas_call | solution.py:454
  52.4 0.0 collective-permute-done.p1_ref
  52.4 0.4 collective-permute-done.1.p2_ref
  52.8 0.0 collective-permute-done.2.p3_ref
  52.9 0.0 copy-done.1
  52.9 0.0 copy-done.2
  52.9 49.8 %mlp_out.1 = bf16[64,512]{1,0:T(8,128)(2,1)S(1)} custom-call(bf16[2048,512]{1,0:T(8,128)(2,1)S(1)} %copy-done.1, bf16[2,1024,512]{2,1,0:T(8,128)(2,1)S(1)} %copy-done.2, bf16[4,2,48,512]{3,2,1,0:T(8,128)(2,1)S(1)} %copy-done.4, bf16[2,128,512]{2,1,0:T(8,128)(2,1)S(1)} %collective-permute-done.p1_ref, bf16[2,128,512]{2,1,0:T(8,128)(2,1)S(1)} %collective-permute-done.1.p2_ref, ...), custom_call_target="tpu_custom_call" | custom-call | flops 12000000000 | bytes 6000000 | tf_op jit(solution)/shard_map/mlp_out/pallas_call | solution.py:630
  102.7 0.6 copy.22
  (14 shorter events, 0.1 us)
Async XLA Ops:
  31.3 21.1 %collective-permute-start = (bf16[2,128,512]{2,1,0:T(8,128)(2,1)}, bf16[2,128,512]{2,1,0:T(8,128)(2,1)S(1)}, u32[]{:S(2)}, u32[]{:S(2)}) collective-permute-start(bf16[2,128,512]{2,1,0:T(8,128)(2,1)} %get-tuple-element.16), channel_id=1, source_target_pairs={{0,8},{8,16},{16,24},{24,0},{1,9},{9,17},{17,25},{25,1},{2,10},{10... | collective-permute-start | bytes 786440 | tf_op jit(solution)/shard_map/ppermute | solution.py:678
  32.7 20.2 %collective-permute-start.1 = (bf16[2,128,512]{2,1,0:T(8,128)(2,1)}, bf16[2,128,512]{2,1,0:T(8,128)(2,1)S(1)}, u32[]{:S(2)}, u32[]{:S(2)}) collective-permute-start(bf16[2,128,512]{2,1,0:T(8,128)(2,1)} %get-tuple-element.17), channel_id=1, source_target_pairs={{0,16},{8,24},{16,0},{24,8},{1,17},{9,25},{17,1},{25,9},{2,18},{10... | collective-permute-start | bytes 786440 | tf_op jit(solution)/shard_map/ppermute | solution.py:678
  35.0 17.9 %collective-permute-start.2 = (bf16[2,128,512]{2,1,0:T(8,128)(2,1)}, bf16[2,128,512]{2,1,0:T(8,128)(2,1)S(1)}, u32[]{:S(2)}, u32[]{:S(2)}) collective-permute-start(bf16[2,128,512]{2,1,0:T(8,128)(2,1)} %get-tuple-element.18), channel_id=1, source_target_pairs={{0,24},{8,0},{16,8},{24,16},{1,25},{9,1},{17,9},{25,17},{2,26},{10... | collective-permute-start | bytes 786440 | tf_op jit(solution)/shard_map/ppermute | solution.py:678
  38.4 0.7 copy-start.6
  39.1 13.8 %copy-start = (bf16[512,64]{0,1:T(8,128)(2,1)S(1)}, bf16[512,64]{0,1:T(8,128)(2,1)}, u32[]{:S(2)}) copy-start(bf16[512,64]{0,1:T(8,128)(2,1)} %param.10) | copy-start | bytes 196612
  39.1 13.8 %copy-start.1 = (bf16[2048,512]{1,0:T(8,128)(2,1)S(1)}, bf16[2048,512]{1,0:T(8,128)(2,1)}, u32[]{:S(2)}) copy-start(bf16[2048,512]{1,0:T(8,128)(2,1)} %get-tuple-element.13.hT) | copy-start | bytes 6291460
  39.1 13.8 %copy-start.2 = (bf16[2,1024,512]{2,1,0:T(8,128)(2,1)S(1)}, bf16[2,1024,512]{2,1,0:T(8,128)(2,1)}, u32[]{:S(2)}) copy-start(bf16[2,1024,512]{2,1,0:T(8,128)(2,1)} %get-tuple-element.14.w2_ref) | copy-start | bytes 6291460
  39.1 13.8 %copy-start.3 = (bf16[1024,512]{1,0:T(8,128)(2,1)S(1)}, bf16[1024,512]{1,0:T(8,128)(2,1)}, u32[]{:S(2)}) copy-start(bf16[1024,512]{1,0:T(8,128)(2,1)} %wd.1) | copy-start | bytes 3145732
  39.1 13.8 %copy-start.4 = (bf16[4,2,48,512]{3,2,1,0:T(8,128)(2,1)S(1)}, bf16[4,2,48,512]{3,2,1,0:T(8,128)(2,1)}, u32[]{:S(2)}) copy-start(bf16[4,2,48,512]{3,2,1,0:T(8,128)(2,1)} %get-tuple-element.15.w1f_ref) | copy-start | bytes 1179652
  39.1 13.8 %copy-start.5 = (bf16[256,512]{1,0:T(8,128)(2,1)S(1)}, bf16[256,512]{1,0:T(8,128)(2,1)}, u32[]{:S(2)}) copy-start(bf16[256,512]{1,0:T(8,128)(2,1)} %wo.1) | copy-start | bytes 786436

commit v2 on v1

--- a/solution.py
+++ b/solution.py
@@ -17,8 +17,8 @@
 NP = 8
 C1A = 16
 C1 = 48
-C2 = 128
-C3 = 80
+C2 = 112
+C3 = 96
 CA = C1 + C2
 CHUNKS = 4
 LANES = 512 // CHUNKS

time: 104 us -> 103 us (level)
  transfers between devices with their start and end apart: 3 -> 3, of which waited for: 1 -> 0; matrix products, arithmetic and copies ran while one was open for 2% -> 2% of each run, Pallas kernels for 13% -> 13%
where the time goes in v2:
time: 103 us
  Pallas kernels  94.1 us (91%)
  starting transfers between devices  4.54 us (4%)
  local copies, waits for them, and re-layouts  2.45 us (2%)
  other arithmetic  1.35 us (1%)
    pallas_call x1, Pallas kernels, call_c(): pl.pallas_call(kernel_c, out_shape=jax.ShapeDtypeStruct((64, 512), BF16),...  49.9 us
    pallas_call x1, Pallas kernels, call_a(): pl.pallas_call(kernel_a, out_shape=(jax.ShapeDtypeStruct((2048, 512), BF1...  30.7 us
    pallas_call x1, Pallas kernels, call_b(): pl.pallas_call(kernel_b, in_specs=[pl.BlockSpec(memory_space=pltpu.SMEM),...  13.5 us
    ppermute x3, starting transfers between devices, local_step(): lax.ppermute(pieces[i], 'x', [(q, (q + i + 1) % NZ) for q in range(NZ)])  4.54 us
  transfers between devices with their start and end apart: 3, of which 0 were waited for; matrix products, arithmetic and copies ran while one was open for 2% of the time, Pallas kernels for 13%

profile of v2, /device:TPU:0, one launch (start us, length us, event | category | flops | bytes accessed | tf_op | source)
XLA Modules:
  0.0 103.3 jit_solution(12148296954748457320)
XLA Ops:
  0.6 30.7 %gather_norm_qkv.1 = (bf16[2048,512]{1,0:T(8,128)(2,1)}, bf16[8,16,288]{2,1,0:T(8,128)(2,1)}, bf16[4,2,48,512]{3,2,1,0:T(8,128)(2,1)}, bf16[2,1024,512]{2,1,0:T(...) custom-call(bf16[64,512]{1,0:T(8,128)(2,1)} %bitcast.12, ...), custom_call_target="tpu_custom_call" | custom-call | tf_op jit(solution)/shard_map/gather_norm_qkv/pallas_call | solution.py:345
  31.3 1.4 %collective-permute-start = (bf16[2,112,512]{2,1,0:T(8,128)(2,1)}, bf16[2,112,512]{2,1,0:T(8,128)(2,1)S(1)}, u32[]{:S(2)}, u32[]{:S(2)}) collective-permute-start(bf16[2,112,512]{2,1,0:T(8,128)(2,1)} %get-tuple-element.16), channel_id=1, source_target_pairs={{0,8},{8,16},{16,24},{24,0},{1,9},{9,17},{17,25},{25,1},{2,10},{10... | collective-permute-start | bytes 688136 | tf_op jit(solution)/shard_map/ppermute | solution.py:678
  32.7 2.3 %collective-permute-start.1 = (bf16[2,112,512]{2,1,0:T(8,128)(2,1)}, bf16[2,112,512]{2,1,0:T(8,128)(2,1)S(1)}, u32[]{:S(2)}, u32[]{:S(2)}) collective-permute-start(bf16[2,112,512]{2,1,0:T(8,128)(2,1)} %get-tuple-element.17), channel_id=1, source_target_pairs={{0,16},{8,24},{16,0},{24,8},{1,17},{9,25},{17,1},{25,9},{2,18},{10... | collective-permute-start | bytes 688136 | tf_op jit(solution)/shard_map/ppermute | solution.py:678
  35.0 0.9 collective-permute-start.2
  35.9 0.9 copy.17
  36.8 0.1 reshape.148
  36.9 0.7 convert_element_type.20
  37.6 0.1 multiply_cosine_fusion
  37.8 0.1 mul.89
  37.8 0.3 subtract_convert_fusion.1
  38.1 0.1 pad_maximum_fusion.1.k_ref
  38.2 0.1 subtract_convert_fusion
  38.3 0.1 pad_maximum_fusion.q_ref
  38.4 0.0 copy-start.6
  38.4 0.6 copy-done.6
  39.1 0.0 copy-start.5
  39.1 13.5 %attend.1 = (bf16[8,16,256]{2,1,0:T(8,128)(2,1)S(1)}, bf16[16,2048,128]{2,1,0:T(8,128)(2,1)}, bf16[16,2048,128]{2,1,0:T(8,128)(2,1)}) custom-call(s32[16]{0:T(128)S(1)} %copy-done.6, bf16[16,16,128]{2,1,0:T(8,128)(2,1)S(1)} %pad_maximum_fusion.q_ref, bf16[16,1,128]{2,1,0:T(2,128)(2,1)S(1)} %pad_maximum_fusion.1.k_ref, bf16[16,1,128]{2,1,0:T(2,128)(2,1)S(1)} %copy.19.v_ref, ...), custom_call_target="tpu_custom_call" | custom-call | flops 12000000000 | bytes 33000000 | tf_op jit(solution)/shard_map/attend/pallas_call | solution.py:454
  52.6 0.0 collective-permute-done.p1_ref
  52.6 0.0 collective-permute-done.1.p2_ref
  52.6 0.0 collective-permute-done.2.p3_ref
  52.7 0.0 copy-done
  52.7 0.0 copy-done.1
  52.7 49.9 %mlp_out.1 = bf16[64,512]{1,0:T(8,128)(2,1)S(1)} custom-call(bf16[2048,512]{1,0:T(8,128)(2,1)S(1)} %copy-done.1, bf16[2,1024,512]{2,1,0:T(8,128)(2,1)S(1)} %copy-done.2, bf16[4,2,48,512]{3,2,1,0:T(8,128)(2,1)S(1)} %copy-done.4, bf16[2,112,512]{2,1,0:T(8,128)(2,1)S(1)} %collective-permute-done.p1_ref, bf16[2,112,512]{2,1,0:T(8,128)(2,1)S(1)} %collective-permute-done.1.p2_ref, ...), custom_call_target="tpu_custom_call" | custom-call | flops 12000000000 | bytes 6000000 | tf_op jit(solution)/shard_map/mlp_out/pallas_call | solution.py:630
  102.7 0.6 copy.22
  (14 shorter events, 0.1 us)
Async XLA Ops:
  31.3 21.3 %collective-permute-start = (bf16[2,112,512]{2,1,0:T(8,128)(2,1)}, bf16[2,112,512]{2,1,0:T(8,128)(2,1)S(1)}, u32[]{:S(2)}, u32[]{:S(2)}) collective-permute-start(bf16[2,112,512]{2,1,0:T(8,128)(2,1)} %get-tuple-element.16), channel_id=1, source_target_pairs={{0,8},{8,16},{16,24},{24,0},{1,9},{9,17},{17,25},{25,1},{2,10},{10... | collective-permute-start | bytes 688136 | tf_op jit(solution)/shard_map/ppermute | solution.py:678
  32.7 20.0 %collective-permute-start.1 = (bf16[2,112,512]{2,1,0:T(8,128)(2,1)}, bf16[2,112,512]{2,1,0:T(8,128)(2,1)S(1)}, u32[]{:S(2)}, u32[]{:S(2)}) collective-permute-start(bf16[2,112,512]{2,1,0:T(8,128)(2,1)} %get-tuple-element.17), channel_id=1, source_target_pairs={{0,16},{8,24},{16,0},{24,8},{1,17},{9,25},{17,1},{25,9},{2,18},{10... | collective-permute-start | bytes 688136 | tf_op jit(solution)/shard_map/ppermute | solution.py:678
  35.0 17.7 %collective-permute-start.2 = (bf16[2,112,512]{2,1,0:T(8,128)(2,1)}, bf16[2,112,512]{2,1,0:T(8,128)(2,1)S(1)}, u32[]{:S(2)}, u32[]{:S(2)}) collective-permute-start(bf16[2,112,512]{2,1,0:T(8,128)(2,1)} %get-tuple-element.18), channel_id=1, source_target_pairs={{0,24},{8,0},{16,8},{24,16},{1,25},{9,1},{17,9},{25,17},{2,26},{10... | collective-permute-start | bytes 688136 | tf_op jit(solution)/shard_map/ppermute | solution.py:678
  38.4 0.7 copy-start.6
  39.1 13.6 %copy-start = (bf16[512,64]{0,1:T(8,128)(2,1)S(1)}, bf16[512,64]{0,1:T(8,128)(2,1)}, u32[]{:S(2)}) copy-start(bf16[512,64]{0,1:T(8,128)(2,1)} %param.10) | copy-start | bytes 196612
  39.1 13.6 %copy-start.1 = (bf16[2048,512]{1,0:T(8,128)(2,1)S(1)}, bf16[2048,512]{1,0:T(8,128)(2,1)}, u32[]{:S(2)}) copy-start(bf16[2048,512]{1,0:T(8,128)(2,1)} %get-tuple-element.13.hT) | copy-start | bytes 6291460
  39.1 13.6 %copy-start.2 = (bf16[2,1024,512]{2,1,0:T(8,128)(2,1)S(1)}, bf16[2,1024,512]{2,1,0:T(8,128)(2,1)}, u32[]{:S(2)}) copy-start(bf16[2,1024,512]{2,1,0:T(8,128)(2,1)} %get-tuple-element.14.w2_ref) | copy-start | bytes 6291460
  39.1 13.6 %copy-start.3 = (bf16[1024,512]{1,0:T(8,128)(2,1)S(1)}, bf16[1024,512]{1,0:T(8,128)(2,1)}, u32[]{:S(2)}) copy-start(bf16[1024,512]{1,0:T(8,128)(2,1)} %wd.1) | copy-start | bytes 3145732
  39.1 13.6 %copy-start.4 = (bf16[4,2,48,512]{3,2,1,0:T(8,128)(2,1)S(1)}, bf16[4,2,48,512]{3,2,1,0:T(8,128)(2,1)}, u32[]{:S(2)}) copy-start(bf16[4,2,48,512]{3,2,1,0:T(8,128)(2,1)} %get-tuple-element.15.w1f_ref) | copy-start | bytes 1179652
  39.1 13.6 %copy-start.5 = (bf16[256,512]{1,0:T(8,128)(2,1)S(1)}, bf16[256,512]{1,0:T(8,128)(2,1)}, u32[]{:S(2)}) copy-start(bf16[256,512]{1,0:T(8,128)(2,1)} %wo.1) | copy-start | bytes 786436
